TPU v7x, 32 devices: a whole 2x2x4 slice. The times are simulated.
32 devices in a mesh: tp: 4 (over z), dp: 8 (over y, x, core).
Axes of the slice: x: 2, y: 2, z: 4, core: 2. Of those that a mesh axis runs over, the one named last changes fastest.
Arguments:
- hidden: bfloat16 [32, 128, 8192], P('dp')
- positions: int32 [128], replicated
- ln1_gain: bfloat16 [8192], replicated
- ln1_bias: bfloat16 [8192], replicated
- w_q: bfloat16 [8192, 8192], P(None, 'tp')
- w_k: bfloat16 [8192, 1024], P(None, 'tp')
- w_v: bfloat16 [8192, 1024], P(None, 'tp')
- w_o: bfloat16 [8192, 8192], P('tp')
- ln2_gain: bfloat16 [8192], replicated
- ln2_bias: bfloat16 [8192], replicated
- w_up: bfloat16 [8192, 32768], P(None, 'tp')
- w_down: bfloat16 [32768, 8192], P('tp')
Outputs:
- output 1: bfloat16 [32, 128, 8192], P('dp')
- output 2: float32 [32768], P('tp')
- output 3: float32 [64], P('tp')
- output 4: float32 [8192], replicated
All inputs are finite; a program needn't handle non-finite values.
Results may differ from a plain program's by a relative error of at most 0.0101556.
Values sent between devices are 32-bit elements.
A program may use at most 1.5 GiB of HBM per device.

v0:
```python
import jax
import jax.numpy as jnp
from jax import lax
from jax.sharding import PartitionSpec as P

HEAD_DIM = 128
ROT_DIM = 64
ROPE_BASE = 10000.0
LN_EPS = 1e-5


def layer_norm_1p(in_rows, ln_gain, ln_bias):
    rows_f32 = in_rows.astype(jnp.float32)
    row_mean = jnp.mean(rows_f32, axis=-1, keepdims=True)
    centered = rows_f32 - row_mean
    row_var = jnp.mean(centered * centered, axis=-1, keepdims=True)
    scaled = centered * lax.rsqrt(row_var + LN_EPS)
    return (scaled * (1.0 + ln_gain.astype(jnp.float32)) + ln_bias.astype(jnp.float32)).astype(jnp.bfloat16)


def rope_tables(positions):
    rot_half = ROT_DIM // 2
    inv_freq = ROPE_BASE ** (-2.0 * jnp.arange(rot_half, dtype=jnp.float32) / ROT_DIM)
    pos_angle = positions.astype(jnp.float32)[:, None] * inv_freq[None, :]
    return jnp.cos(pos_angle), jnp.sin(pos_angle)


def apply_rope(heads_in, cos_b, sin_b):
    rot_half = ROT_DIM // 2
    heads_f32 = heads_in.astype(jnp.float32)
    lead_half = heads_f32[..., :rot_half]
    tail_half = heads_f32[..., rot_half:ROT_DIM]
    turned = jnp.concatenate([lead_half * cos_b - tail_half * sin_b, tail_half * cos_b + lead_half * sin_b], axis=-1)
    return jnp.concatenate([turned.astype(jnp.bfloat16), heads_in[..., ROT_DIM:]], axis=-1)


def attention_block(h_in, positions, w_q, w_k, w_v):
    n_batch = h_in.shape[0]
    n_seq = h_in.shape[1]
    kv_heads = w_k.shape[1] // HEAD_DIM
    q_group = w_q.shape[1] // w_k.shape[1]
    cos_t, sin_t = rope_tables(positions)
    q_proj = jnp.einsum("bsd,dn->bsn", h_in, w_q, preferred_element_type=jnp.float32).astype(jnp.bfloat16)
    q_proj = q_proj.reshape(n_batch, n_seq, kv_heads, q_group, HEAD_DIM)
    k_proj = jnp.einsum("bsd,dn->bsn", h_in, w_k, preferred_element_type=jnp.float32).astype(jnp.bfloat16)
    k_proj = k_proj.reshape(n_batch, n_seq, kv_heads, HEAD_DIM)
    v_proj = jnp.einsum("bsd,dn->bsn", h_in, w_v, preferred_element_type=jnp.float32).astype(jnp.bfloat16)
    v_proj = v_proj.reshape(n_batch, n_seq, kv_heads, HEAD_DIM)
    q_proj = apply_rope(q_proj, cos_t[None, :, None, None, :], sin_t[None, :, None, None, :])
    k_proj = apply_rope(k_proj, cos_t[None, :, None, :], sin_t[None, :, None, :])
    scores = jnp.einsum("bqkgd,bskd->bkgqs", q_proj, k_proj, preferred_element_type=jnp.float32) * HEAD_DIM ** -0.5
    causal = jnp.arange(n_seq)[:, None] >= jnp.arange(n_seq)[None, :]
    scores = jnp.where(causal, scores, -1e30)
    attn_prob = jax.nn.softmax(scores, axis=-1).astype(jnp.bfloat16)
    return jnp.einsum("bkgqs,bskd->bqkgd", attn_prob, v_proj, preferred_element_type=jnp.float32).astype(jnp.bfloat16)


def solution(mesh):
    def local_layer(hidden, positions, ln1_gain, ln1_bias, w_q, w_k, w_v, w_o, ln2_gain, ln2_bias, w_up, w_down):
        n_batch = hidden.shape[0]
        n_seq = hidden.shape[1]
        h_in = layer_norm_1p(hidden, ln1_gain, ln1_bias)
        attn_out = attention_block(h_in, positions, w_q, w_k, w_v)
        head_norm = jnp.sqrt(jnp.sum(jnp.square(attn_out.astype(jnp.float32)), axis=-1)).reshape(n_batch, n_seq, -1)
        o_part = jnp.einsum("bsn,nd->bsd", attn_out.reshape(n_batch, n_seq, -1), w_o, preferred_element_type=jnp.float32)
        o_sum = lax.psum(o_part, "tp")
        x_mid = (hidden.astype(jnp.float32) + o_sum).astype(jnp.bfloat16)
        h_mid = layer_norm_1p(x_mid, ln2_gain, ln2_bias)
        mlp_act = jnp.square(jax.nn.relu(jnp.einsum("bsd,df->bsf", h_mid, w_up, preferred_element_type=jnp.float32)))
        mlp_part = jnp.einsum("bsf,fd->bsd", mlp_act.astype(jnp.bfloat16), w_down, preferred_element_type=jnp.float32)
        mlp_sum = lax.psum(mlp_part, "tp")
        out_hidden = (x_mid.astype(jnp.float32) + mlp_sum).astype(jnp.bfloat16)
        neuron_sq = jnp.sum(jnp.square(jnp.mean(mlp_act, axis=1)), axis=0)
        head_sq = jnp.sum(jnp.square(jnp.mean(head_norm, axis=1)), axis=0)
        ln1_sq = jnp.sum(jnp.square(jnp.mean(h_in, axis=1, dtype=jnp.float32)), axis=0)
        ln2_sq = jnp.sum(jnp.square(jnp.mean(h_mid, axis=1, dtype=jnp.float32)), axis=0)
        packed = jnp.concatenate([neuron_sq, head_sq, ln1_sq + ln2_sq])
        score_roots = jnp.sqrt(lax.psum(packed, "dp"))
        ff_local = neuron_sq.shape[0]
        heads_local = head_sq.shape[0]
        f_neuron = score_roots[:ff_local]
        f_head = score_roots[ff_local:ff_local + heads_local]
        f_embed = score_roots[ff_local + heads_local:]
        return out_hidden, f_neuron, f_head, f_embed

    weight_col = P(None, "tp")
    weight_row = P("tp", None)
    return jax.shard_map(
        local_layer,
        mesh=mesh,
        in_specs=(P("dp"), P(), P(), P(), weight_col, weight_col, weight_col, weight_row, P(), P(), weight_col, weight_row),
        out_specs=(P("dp"), P("tp"), P("tp"), P()),
        check_vma=False,
    )
```

profile of v0, /device:TPU:0, one launch (start us, length us, event | category | flops | bytes accessed | tf_op | source)
XLA Modules:
  0.0 1464.1 jit_solution(11095615427289697306)
XLA Ops:
  7.3 4.7 convert_reduce_fusion.1
  12.0 1.0 copy-done.1
  13.0 2.3 fusion.17
  15.4 23.1 %fusion.33 = bf16[4,128,2048]{2,1,0:T(8,128)(2,1)S(1)} fusion(bf16[8192,2048]{1,0:T(8,128)(2,1)} %param.16, bf16[4,128,8192]{2,1,0:T(8,128)(2,1)S(1)} %copy-done.1, f32[8192]{0:T(1024)S(1)} %convert_element_type.75, f32[8192]{0:T(1024)S(1)} %convert_add_fusion.3, f32[4,128]{1,0:T(4,128)S(1)} %add_rsqrt_fusion.1, f32[4,128]{1,0:T(4,128)S(1)} %broadcast_multiply_fusion.1), kind=kOutput, calls=%fused_computation.46 | convolution fusion | flops 17206083584 | bytes 44109824 | tf_op jit(solution)/shard_map/bsd,dn->bsn/dot_general | solution.py:43
  38.4 0.6 copy.59
  39.1 0.6 slice.41
  39.7 2.6 copy_convert_fusion
  42.3 3.6 fusion.53
  46.0 3.7 fusion.47
  50.1 0.5 copy.69
  50.6 0.3 multiply_cosine_fusion
  51.2 0.8 copy-done.2
  52.0 1.5 subtract_convert_fusion
  53.5 2.6 fusion.36
  56.1 1.1 fusion.72
  57.2 1.5 multiply_reduce_fusion
  58.7 27.1 %fusion.5 = f32[4,128,8192]{2,1,0:T(8,128)} fusion(bf16[4,128,2048]{1,2,0:T(8,128)(2,1)S(1)} %bitcast.71, bf16[2048,8192]{1,0:T(8,128)(2,1)} %param.19), kind=kOutput, calls=%fused_computation.5 | convolution fusion | flops 17179869184 | bytes 52428800 | tf_op jit(solution)/shard_map/bsn,nd->bsd/dot_general | solution.py:65
  85.9 0.6 copy-done.7
  86.6 561.7 %all-reduce.4.cloned.1.call-done = f32[4,128,8192]{2,1,0:T(8,128)} async-done(((f32[4,128,8192]{2,1,0:T(8,128)}), f32[4,128,8192]{2,1,0:T(8,128)}) %all-reduce.4.cloned.1.call-update) | async-done | bytes 16777232 | tf_op jit(solution)/shard_map/psum | solution.py:66
  648.3 11.6 convert_reduce_fusion
  660.0 3.4 copy-done
  663.4 2.3 fusion.13
  665.7 80.8 %fusion.23 = (f32[4,8192]{1,0:T(4,128)S(1)}, f32[4,128,8192]{2,1,0:T(8,128)}) fusion(bf16[8192,8192]{1,0:T(8,128)(2,1)} %param.22, bf16[4,128,8192]{2,1,0:T(8,128)(2,1)} %copy-done, f32[8192]{0:T(1024)S(1)} %convert_element_type.89, f32[8192]{0:T(1024)S(1)} %convert_add_fusion.2, f32[4,128]{1,0:T(4,128)S(1)} %add_rsqrt_fusion, ...), kind=kOutput, calls=%fused_computation.32 | convolution fusion | flops 68757192704 | bytes 159584256 | tf_op jit(solution)/shard_map/bsd,df->bsf/dot_general | solution.py:69
  746.4 84.1 %fusion.1 = f32[4,128,8192]{2,1,0:T(8,128)} fusion(bf16[8192,8192]{1,0:T(8,128)(2,1)} %param.23, f32[4,128,8192]{2,1,0:T(8,128)} %get-tuple-element.22), kind=kOutput, calls=%fused_computation.1 | convolution fusion | flops 68732059648 | bytes 167772160 | tf_op jit(solution)/shard_map/bsf,fd->bsd/dot_general | solution.py:70
  830.6 0.7 copy-done.4
  831.6 557.6 %all-reduce.6.cloned.1.call-done = f32[4,128,8192]{2,1,0:T(8,128)} async-done(((f32[4,128,8192]{2,1,0:T(8,128)}), f32[4,128,8192]{2,1,0:T(8,128)}) %all-reduce.6.cloned.1.call-update) | async-done | bytes 16777232 | tf_op jit(solution)/shard_map/psum | solution.py:71
  1389.2 12.6 convert_reduce_fusion.2
  1402.0 0.7 concatenate.17
  1402.7 52.3 %all-reduce.8.cloned.1.call-done = f32[16400]{0:T(1024)} async-done(((f32[16400]{0:T(1024)}), f32[16400]{0:T(1024)}) %all-reduce.8.cloned.1.call-update) | async-done | bytes 65616 | tf_op jit(solution)/shard_map/psum | solution.py:78
  1454.9 0.9 sqrt.9
  1455.8 0.5 slice.43
  1456.4 0.7 fusion.71
  (46 shorter events, 1.4 us)
Async XLA Ops:
  7.2 641.2 %all-reduce.4.cloned.1.call-start = ((), (), s32[]{:S(2)}) async-start(), calls=%async_computation | async-start | bytes 33554432 | tf_op jit(solution)/shard_map/psum | solution.py:66
  7.2 5.8 copy-start.1
  7.3 8.1 copy-start.5
  7.3 8.1 copy-start.6
  38.4 3.9 copy-start.11
  38.4 3.9 copy-start.9
  42.3 3.7 copy-start.10
  49.8 2.2 copy-start.2
  85.8 0.7 copy-start.7
  85.8 0.7 copy-start.8
  85.9 1303.3 %all-reduce.6.cloned.1.call-start = ((), (), s32[]{:S(2)}) async-start(), calls=%async_computation.1 | async-start | bytes 33554432 | tf_op jit(solution)/shard_map/psum | solution.py:71
  660.0 3.4 copy-start
  830.5 0.8 copy-start.4
  830.5 624.4 %all-reduce.8.cloned.1.call-start = ((), (), s32[]{:S(2)}) async-start(), calls=%async_computation.2 | async-start | bytes 139264 | tf_op jit(solution)/shard_map/psum | solution.py:78
  831.6 570.2 %copy-start.3 = (f32[4,8192]{1,0:T(4,128)S(1)}, f32[4,8192]{1,0:T(4,128)}, u32[]{:S(2)}) copy-start(f32[4,8192]{1,0:T(4,128)} %get-tuple-element.8) | copy-start | bytes 393220
Sparse Core Ops, SparseCore 0:
  86.0 562.2 all-reduce.3
  830.7 558.4 all-reduce.5
  1402.8 52.0 all-reduce.7
where the time goes:
time: 1470 us; the launch traced here: 1460 us
  waiting for transfers between devices  1170 us (80%)
  matrix products  226 us (15%)
  other arithmetic  39.8 us (3%)
    psum x1, waiting for transfers between devices, local_layer(): o_sum = lax.psum(o_part, 'tp')  562 us
    psum x1, waiting for transfers between devices, local_layer(): mlp_sum = lax.psum(mlp_part, 'tp')  558 us
    dot_general x1, matrix products, local_layer(): jnp.einsum('bsf,fd->bsd', mlp_act.astype(jnp.bfloat16), w_down, preferred...  84.1 us
    dot_general x1, matrix products, local_layer(): jnp.einsum('bsd,df->bsf', h_mid, w_up, preferred_element_type=jnp.float32)  80.8 us
    psum x1, waiting for transfers between devices, local_layer(): score_roots = jnp.sqrt(lax.psum(packed, 'dp'))  52.3 us
  transfers between devices with their start and end apart: 3, of which 3 were waited for; matrix products, arithmetic and copies ran while one was open for 0% of the time, Pallas kernels for 0%

commit v1 on v0

--- a/solution.py
+++ b/solution.py
@@ -1,12 +1,22 @@
+import functools
+
 import jax
 import jax.numpy as jnp
 from jax import lax
+from jax.experimental import pallas as pl
+from jax.experimental.pallas import tpu as pltpu
 from jax.sharding import PartitionSpec as P
 
 HEAD_DIM = 128
 ROT_DIM = 64
 ROPE_BASE = 10000.0
 LN_EPS = 1e-5
+MESH = pl.DeviceIdType.MESH
+
+ITEM_COLS = 256
+SKEW = 2
+SLOTS = 8
+LN_PARTS = 4
 
 
 def layer_norm_1p(in_rows, ln_gain, ln_bias):
@@ -55,33 +65,449 @@
     return jnp.einsum("bkgqs,bskd->bqkgd", attn_prob, v_proj, preferred_element_type=jnp.float32).astype(jnp.bfloat16)
 
 
+def tail_kernel(
+    dims,
+    attn_hbm, x_hbm, wo_hbm, wup_hbm, wdn_hbm, gain_ref, bias_ref, pay_in,
+    y_hbm, score_ref,
+    attn, xbuf, part, lhs, wbuf, rslot, bslot, acc8, pay, recvpay,
+    in_sem, w_sem, r_send, r_recv, b_send, b_recv, p_send, p_recv, r_cred, b_cred,
+):
+    tp, dp, n_seq, width, k_attn, n_items, n_chunks = dims
+    z = lax.axis_index("tp")
+    d = lax.axis_index("dp")
+    last = tp - 1
+    cw = width // n_items
+    bw = 2 * cw
+    n_blk = width // bw
+    rows = 2 * n_seq
+    total = 2 * n_chunks * n_items
+    lag = 2 * last * SKEW
+
+    barrier = pltpu.get_barrier_semaphore()
+    for o in range(1, tp):
+        pl.semaphore_signal(barrier, inc=1, device_id={"tp": lax.rem(z + o, tp)}, device_id_type=MESH)
+    for o in range(1, dp):
+        pl.semaphore_signal(barrier, inc=1, device_id={"dp": lax.rem(d + o, dp)}, device_id_type=MESH)
+
+    attn_copy = pltpu.make_async_copy(attn_hbm, attn, in_sem.at[0])
+    x_copy = pltpu.make_async_copy(x_hbm, xbuf, in_sem.at[1])
+
+    def wo_copy(b, slot):
+        cols = pl.ds(pl.multiple_of(b * bw, bw), bw)
+        return pltpu.make_async_copy(wo_hbm.at[:, cols], wbuf.at[slot, pl.ds(0, k_attn), :], w_sem.at[slot])
+
+    def w_copy(hbm, b, slot):
+        cols = pl.ds(pl.multiple_of(b * bw, bw), bw)
+        return pltpu.make_async_copy(hbm.at[:, cols], wbuf.at[slot], w_sem.at[slot])
+
+    def start_w(k):
+        slot = lax.rem(k, 2)
+        kk = lax.rem(k, 2 * n_blk)
+
+        @pl.when(kk < n_blk)
+        def _():
+            w_copy(wup_hbm, kk, slot).start()
+
+        @pl.when(kk >= n_blk)
+        def _():
+            w_copy(wdn_hbm, kk - n_blk, slot).start()
+
+    def out_proj(b):
+        slot = lax.rem(b, 2)
+        wo_copy(b, slot).wait()
+        acc = jnp.dot(attn[...], wbuf[slot, 0:k_attn, :], preferred_element_type=jnp.float32)
+        for c in range(n_chunks):
+            for g in range(2):
+                for half in range(2):
+                    r0 = (2 * c + g) * n_seq
+                    part[(2 * c + g) * n_items + 2 * b + half] = acc[r0:r0 + n_seq, half * cw:(half + 1) * cw]
+
+        @pl.when(b + 2 < n_blk)
+        def _():
+            wo_copy(b + 2, slot).start()
+
+        @pl.when(b + 2 >= n_blk)
+        def _():
+            start_w(b + 2 - n_blk)
+
+    attn_copy.start()
+    wo_copy(0, 0).start()
+    wo_copy(1, 1).start()
+    x_copy.start()
+    pay[...] = pay_in[...]
+    attn_copy.wait()
+    out_proj(0)
+    x_copy.wait()
+    pl.semaphore_wait(barrier, tp - 1 + dp - 1)
+
+    def tile_of(t, g):
+        c = lax.rem(lax.div(t, n_items), n_chunks)
+        i = lax.rem(t, n_items)
+        row = pl.multiple_of((2 * c + g) * n_seq, n_seq)
+        col = pl.multiple_of(i * cw, cw)
+        return (2 * c + g) * n_items + i, pl.ds(row, n_seq), pl.ds(col, cw)
+
+    def place(g):
+        return z if g == 0 else last - z
+
+    def onward(g):
+        return {"tp": z + 1} if g == 0 else {"tp": z - 1}
+
+    def backward(g):
+        return {"tp": z - 1} if g == 0 else {"tp": z + 1}
+
+    def r_copy(g, t, src):
+        slot = lax.rem(t, SLOTS)
+        return pltpu.make_async_remote_copy(
+            src_ref=src, dst_ref=rslot.at[g, slot], send_sem=r_send.at[g, slot], recv_sem=r_recv.at[g, slot],
+            device_id=onward(g), device_id_type=MESH,
+        )
+
+    def b_copy(g, t, src):
+        slot = lax.rem(t, SLOTS)
+        return pltpu.make_async_remote_copy(
+            src_ref=src, dst_ref=bslot.at[g, slot], send_sem=b_send.at[g, slot], recv_sem=b_recv.at[g, slot],
+            device_id=backward(g), device_id_type=MESH,
+        )
+
+    def r_arrive(g, t, p):
+        slot = lax.rem(t, SLOTS)
+        idx, rws, cls = tile_of(t, g)
+
+        @pl.when((p == 1) | (p == 2))
+        def _():
+            r_copy(g, t, rslot.at[g, slot]).wait_recv()
+            rslot[g, slot] = rslot[g, slot] + part[idx]
+
+        @pl.when(p == last)
+        def _():
+            r_copy(g, t, rslot.at[g, slot]).wait_recv()
+            new = (xbuf[rws, cls].astype(jnp.float32) + (rslot[g, slot] + part[idx])).astype(jnp.bfloat16)
+            xbuf[rws, cls] = new
+            rslot[g, slot] = new.astype(jnp.float32)
+
+    def r_leave(g, t, p):
+        slot = lax.rem(t, SLOTS)
+        old = t - SKEW
+        old_slot = lax.rem(old + SLOTS, SLOTS)
+        idx, _, _ = tile_of(t, g)
+
+        @pl.when((p == 0) & (t >= SLOTS))
+        def _():
+            r_copy(g, t, part.at[idx]).wait_send()
+
+        @pl.when((p < last) & (t >= SLOTS))
+        def _():
+            pl.semaphore_wait(r_cred.at[g], 1)
+
+        @pl.when(p == 0)
+        def _():
+            r_copy(g, t, part.at[idx]).start()
+
+        @pl.when((p == 1) | (p == 2))
+        def _():
+            r_copy(g, t, rslot.at[g, slot]).start()
+
+        @pl.when((p == last) & (t >= SLOTS))
+        def _():
+            pl.semaphore_wait(b_cred.at[g], 1)
+
+        @pl.when(p == last)
+        def _():
+            b_copy(g, t, rslot.at[g, slot]).start()
+
+        @pl.when(((p == 1) | (p == 2)) & (old >= 0))
+        def _():
+            r_copy(g, old, rslot.at[g, old_slot]).wait_send()
+
+        @pl.when((p == last) & (old >= 0))
+        def _():
+            b_copy(g, old, rslot.at[g, old_slot]).wait_send()
+
+        @pl.when((p > 0) & (old >= 0) & (old < total - SLOTS))
+        def _():
+            pl.semaphore_signal(r_cred.at[g], inc=1, device_id=backward(g), device_id_type=MESH)
+
+    def b_step(g, t, p):
+        slot = lax.rem(t, SLOTS)
+        old = t - SKEW
+        old_slot = lax.rem(old + SLOTS, SLOTS)
+        _, rws, cls = tile_of(t, g)
+        b_copy(g, t, bslot.at[g, slot]).wait_recv()
+
+        @pl.when((p > 0) & (t >= SLOTS))
+        def _():
+            pl.semaphore_wait(b_cred.at[g], 1)
+
+        @pl.when(p > 0)
+        def _():
+            b_copy(g, t, bslot.at[g, slot]).start()
+
+        xbuf[rws, cls] = bslot[g, slot].astype(jnp.bfloat16)
+
+        @pl.when((p > 0) & (old >= 0))
+        def _():
+            b_copy(g, old, bslot.at[g, old_slot]).wait_send()
+
+        @pl.when((old >= 0) & (old < total - SLOTS))
+        def _():
+            pl.semaphore_signal(b_cred.at[g], inc=1, device_id=onward(g), device_id_type=MESH)
+
+    def service(s):
+        for g in range(2):
+            p = place(g)
+            t = s - SKEW * p
+
+            @pl.when((t >= 0) & (t < total))
+            def _(g=g, p=p, t=t):
+                r_arrive(g, t, p)
+
+        for g in range(2):
+            p = place(g)
+            t = s - SKEW * (2 * last - p)
+
+            @pl.when((p < last) & (t >= 0) & (t < total))
+            def _(g=g, p=p, t=t):
+                b_step(g, t, p)
+
+        for g in range(2):
+            p = place(g)
+            t = s - SKEW * p
+
+            @pl.when((t >= 0) & (t < total))
+            def _(g=g, p=p, t=t):
+                r_leave(g, t, p)
+
+    lane = 512 if width % 512 == 0 else 128
+    n_lane = width // lane
+    ln_rows = rows // LN_PARTS
+    seq_parts = n_seq // ln_rows
+
+    def ln_part(c, q):
+        @pl.when(lax.rem(q, seq_parts) == 0)
+        def _():
+            acc8[...] = jnp.zeros_like(acc8)
+
+        def group(r, carry):
+            src = pl.ds(pl.multiple_of(c * rows + q * ln_rows + r * 16, 16), 16)
+            dst = pl.ds(pl.multiple_of(q * ln_rows + r * 16, 16), 16)
+            tot = jnp.zeros((16, lane), jnp.float32)
+            for j in range(n_lane):
+                tot = tot + xbuf[src, j * lane:(j + 1) * lane].astype(jnp.float32)
+            mean = jnp.sum(tot, axis=-1, keepdims=True) * (1.0 / width)
+            var = jnp.zeros((16, lane), jnp.float32)
+            for j in range(n_lane):
+                cen = xbuf[src, j * lane:(j + 1) * lane].astype(jnp.float32) - mean
+                var = var + cen * cen
+            rstd = lax.rsqrt(jnp.sum(var, axis=-1, keepdims=True) * (1.0 / width) + LN_EPS)
+            for j in range(n_lane):
+                cl = slice(j * lane, (j + 1) * lane)
+                cen = xbuf[src, cl].astype(jnp.float32) - mean
+                h = ((cen * rstd) * (1.0 + gain_ref[:, cl]) + bias_ref[:, cl]).astype(jnp.bfloat16)
+                lhs[0, dst, cl] = h
+                hf = h.astype(jnp.float32)
+                acc8[:, cl] = acc8[:, cl] + (hf[0:8] + hf[8:16])
+            return carry
+
+        lax.fori_loop(0, ln_rows // 16, group, 0)
+
+        @pl.when(lax.rem(q, seq_parts) == seq_parts - 1)
+        def _():
+            m = jnp.sum(acc8[...], axis=0, keepdims=True) * (1.0 / n_seq)
+            pay[:, width:2 * width] = pay[:, width:2 * width] + m * m
+
+    def mlp_block(k):
+        slot = lax.rem(k, 2)
+        kk = lax.rem(k, 2 * n_blk)
+        c = lax.div(k, 2 * n_blk)
+        second = lax.div(kk, n_blk)
+        b = kk - second * n_blk
+        w_copy(wup_hbm, b, slot).wait()
+        acc = jnp.dot(lhs[second], wbuf[slot], preferred_element_type=jnp.float32)
+
+        @pl.when(second == 0)
+        def _():
+            relu = jnp.maximum(acc, 0.0)
+            act = relu * relu
+            cols = pl.ds(pl.multiple_of(b * bw, bw), bw)
+            m0 = jnp.sum(act[0:n_seq], axis=0, keepdims=True) * (1.0 / n_seq)
+            m1 = jnp.sum(act[n_seq:rows], axis=0, keepdims=True) * (1.0 / n_seq)
+            pay[:, cols] = pay[:, cols] + (m0 * m0 + m1 * m1)
+            lhs[1, :, cols] = act.astype(jnp.bfloat16)
+
+        @pl.when(second == 1)
+        def _():
+            for g in range(2):
+                for half in range(2):
+                    part[(2 * c + g) * n_items + 2 * b + half] = acc[
+                        g * n_seq:(g + 1) * n_seq, half * cw:(half + 1) * cw
+                    ]
+
+        @pl.when(k + 2 < 2 * n_blk * n_chunks)
+        def _():
+            start_w(k + 2)
+
+    def pay_copy(peer, src_d, o):
+        return pltpu.make_async_remote_copy(
+            src_ref=pay, dst_ref=recvpay.at[src_d], send_sem=p_send.at[o], recv_sem=p_recv.at[src_d],
+            device_id={"dp": peer}, device_id_type=MESH,
+        )
+
+    def y_copy(c):
+        r = pl.ds(c * rows, rows)
+        return pltpu.make_async_copy(xbuf.at[r, :], y_hbm.at[r, :], in_sem.at[c])
+
+    ln_at = n_items - 1 + lag
+    mlp_at = ln_at + LN_PARTS
+    n_mlp = 2 * n_blk * n_chunks
+    pay_at = mlp_at + n_mlp - n_blk + 2
+
+    def step(s, carry):
+        service(s)
+
+        @pl.when(s + 1 < n_blk)
+        def _():
+            out_proj(s + 1)
+
+        for c in range(n_chunks):
+            q = s - ln_at - c * n_items
+
+            @pl.when((q >= 0) & (q < LN_PARTS))
+            def _(c=c, q=q):
+                ln_part(c, q)
+
+        k = s - mlp_at
+
+        @pl.when((k >= 0) & (k < n_mlp))
+        def _():
+            mlp_block(k)
+
+        @pl.when(s == pay_at)
+        def _():
+            for o in range(1, dp):
+                pay_copy(lax.rem(d + o, dp), d, o).start()
+            recvpay[d] = pay[...]
+
+        for c in range(n_chunks - 1):
+            @pl.when(s == total - 1 + lag - (n_chunks - 1 - c) * n_items)
+            def _(c=c):
+                y_copy(c).start()
+
+        return carry
+
+    lax.fori_loop(0, total + lag, step, 0)
+
+    y_copy(n_chunks - 1).start()
+    for o in range(1, dp):
+        src_d = lax.rem(d + o, dp)
+        pay_copy(src_d, src_d, o).wait_recv()
+    score = recvpay[0]
+    for j in range(1, dp):
+        score = score + recvpay[j]
+    score_ref[...] = score
+    for o in range(1, dp):
+        pay_copy(lax.rem(d + o, dp), d, o).wait_send()
+    for g in range(2):
+        p = place(g)
+        for back in range(SLOTS):
+            t = total - 1 - back
+            slot = t % SLOTS
+
+            @pl.when(p == 0)
+            def _(g=g, t=t, slot=slot):
+                r_copy(g, t, part.at[0]).wait_send()
+
+            if back < SKEW:
+                @pl.when((p == 1) | (p == 2))
+                def _(g=g, t=t, slot=slot):
+                    r_copy(g, t, rslot.at[g, slot]).wait_send()
+                    b_copy(g, t, bslot.at[g, slot]).wait_send()
+
+                @pl.when(p == last)
+                def _(g=g, t=t, slot=slot):
+                    b_copy(g, t, rslot.at[g, slot]).wait_send()
+    for c in range(n_chunks):
+        y_copy(c).wait()
+
+
+def layer_tail(tp, dp, attn, x_rows, w_o, w_up, w_down, gain, bias, pay, n_seq):
+    tokens, width = x_rows.shape
+    k_attn = attn.shape[1]
+    n_items = width // ITEM_COLS
+    n_chunks = tokens // (2 * n_seq)
+    dims = (tp, dp, n_seq, width, k_attn, n_items, n_chunks)
+    cw = ITEM_COLS
+    hbm = pl.BlockSpec(memory_space=pl.ANY)
+    vmem = pl.BlockSpec(memory_space=pltpu.VMEM)
+    dma = pltpu.SemaphoreType.DMA
+    return pl.pallas_call(
+        functools.partial(tail_kernel, dims),
+        name="layer_tail",
+        out_shape=(
+            jax.ShapeDtypeStruct((tokens, width), jnp.bfloat16),
+            jax.ShapeDtypeStruct(pay.shape, jnp.float32),
+        ),
+        in_specs=[hbm, hbm, hbm, hbm, hbm, vmem, vmem, vmem],
+        out_specs=(hbm, vmem),
+        scratch_shapes=[
+            pltpu.VMEM((tokens, k_attn), jnp.bfloat16),
+            pltpu.VMEM((tokens, width), jnp.bfloat16),
+            pltpu.VMEM((2 * n_chunks * n_items, n_seq, cw), jnp.float32),
+            pltpu.VMEM((2, 2 * n_seq, width), jnp.bfloat16),
+            pltpu.VMEM((2, width, 2 * cw), jnp.bfloat16),
+            pltpu.VMEM((2, SLOTS, n_seq, cw), jnp.float32),
+            pltpu.VMEM((2, SLOTS, n_seq, cw), jnp.float32),
+            pltpu.VMEM((8, width), jnp.float32),
+            pltpu.VMEM(pay.shape, jnp.float32),
+            pltpu.VMEM((dp,) + pay.shape, jnp.float32),
+            dma((2,)), dma((2,)),
+            dma((2, SLOTS)), dma((2, SLOTS)), dma((2, SLOTS)), dma((2, SLOTS)),
+            dma((dp,)), dma((dp,)),
+            pltpu.SemaphoreType.REGULAR((2,)), pltpu.SemaphoreType.REGULAR((2,)),
+        ],
+        compiler_params=pltpu.CompilerParams(
+            collective_id=0, has_side_effects=True, vmem_limit_bytes=66_000_000
+        ),
+        cost_estimate=pl.CostEstimate(
+            flops=2 * tokens * width * (k_attn + 2 * width),
+            bytes_accessed=2 * width * (k_attn + 4 * width),
+            transcendentals=0,
+        ),
+    )(attn, x_rows, w_o, w_up, w_down, gain, bias, pay)
+
+
 def solution(mesh):
+    tp = mesh.shape["tp"]
+    dp = mesh.shape["dp"]
+
     def local_layer(hidden, positions, ln1_gain, ln1_bias, w_q, w_k, w_v, w_o, ln2_gain, ln2_bias, w_up, w_down):
-        n_batch = hidden.shape[0]
-        n_seq = hidden.shape[1]
+        n_batch, n_seq, width = hidden.shape
+        ff_local = w_up.shape[1]
         h_in = layer_norm_1p(hidden, ln1_gain, ln1_bias)
         attn_out = attention_block(h_in, positions, w_q, w_k, w_v)
         head_norm = jnp.sqrt(jnp.sum(jnp.square(attn_out.astype(jnp.float32)), axis=-1)).reshape(n_batch, n_seq, -1)
-        o_part = jnp.einsum("bsn,nd->bsd", attn_out.reshape(n_batch, n_seq, -1), w_o, preferred_element_type=jnp.float32)
-        o_sum = lax.psum(o_part, "tp")
-        x_mid = (hidden.astype(jnp.float32) + o_sum).astype(jnp.bfloat16)
-        h_mid = layer_norm_1p(x_mid, ln2_gain, ln2_bias)
-        mlp_act = jnp.square(jax.nn.relu(jnp.einsum("bsd,df->bsf", h_mid, w_up, preferred_element_type=jnp.float32)))
-        mlp_part = jnp.einsum("bsf,fd->bsd", mlp_act.astype(jnp.bfloat16), w_down, preferred_element_type=jnp.float32)
-        mlp_sum = lax.psum(mlp_part, "tp")
-        out_hidden = (x_mid.astype(jnp.float32) + mlp_sum).astype(jnp.bfloat16)
-        neuron_sq = jnp.sum(jnp.square(jnp.mean(mlp_act, axis=1)), axis=0)
         head_sq = jnp.sum(jnp.square(jnp.mean(head_norm, axis=1)), axis=0)
         ln1_sq = jnp.sum(jnp.square(jnp.mean(h_in, axis=1, dtype=jnp.float32)), axis=0)
-        ln2_sq = jnp.sum(jnp.square(jnp.mean(h_mid, axis=1, dtype=jnp.float32)), axis=0)
-        packed = jnp.concatenate([neuron_sq, head_sq, ln1_sq + ln2_sq])
-        score_roots = jnp.sqrt(lax.psum(packed, "dp"))
-        ff_local = neuron_sq.shape[0]
-        heads_local = head_sq.shape[0]
-        f_neuron = score_roots[:ff_local]
-        f_head = score_roots[ff_local:ff_local + heads_local]
-        f_embed = score_roots[ff_local + heads_local:]
-        return out_hidden, f_neuron, f_head, f_embed
+        heads = head_sq.shape[0]
+        pay = jnp.concatenate(
+            [jnp.zeros((ff_local,), jnp.float32), ln1_sq, head_sq, jnp.zeros((128 - heads,), jnp.float32)]
+        ).reshape(1, -1)
+        y_rows, score = layer_tail(
+            tp, dp,
+            attn_out.reshape(n_batch * n_seq, -1),
+            hidden.reshape(n_batch * n_seq, width),
+            w_o, w_up, w_down,
+            ln2_gain.astype(jnp.float32).reshape(1, width),
+            ln2_bias.astype(jnp.float32).reshape(1, width),
+            pay, n_seq,
+        )
+        roots = jnp.sqrt(score.reshape(-1))
+        return (
+            y_rows.reshape(n_batch, n_seq, width),
+            roots[:ff_local],
+            roots[ff_local + width:ff_local + width + heads],
+            roots[ff_local:ff_local + width],
+        )
 
     weight_col = P(None, "tp")
     weight_row = P("tp", None)

time: 1470 us -> 824 us (0.56)
  waiting for transfers between devices: 1170 us -> 0 us
  Pallas kernels: 0 us -> 749 us
  matrix products: 226 us -> 36.4 us
  other arithmetic: 39.8 us -> 18 us
    psum x3 -> x0, waiting for transfers between devices: 1170 us -> none  [the longest x1 562 us: local_layer(): o_sum = lax.psum(o_part, 'tp')]
    pallas_call x0 -> x1, Pallas kernels: none -> 749 us  [layer_tail(): pl.pallas_call(functools.partial(tail_kernel, dims), name='layer_tail', o...]
    dot_general x3 -> x0, matrix products: 192 us -> none  [the longest x1 84.1 us: local_layer(): jnp.einsum('bsf,fd->bsd', mlp_act.astype(jnp.bfloat16), w_down, preferred...]
  transfers between devices with their start and end apart: 3 -> 0, of which waited for: 3 -> 0; matrix products, arithmetic and copies ran while one was open for 0% -> 0% of each run, Pallas kernels for 0% -> 0%
where the time goes in v1:
time: 824 us
  Pallas kernels  749 us (91%)
  matrix products  36.4 us (4%)
  local copies, waits for them, and re-layouts  19.7 us (2%)
  other arithmetic  18 us (2%)
    pallas_call x1, Pallas kernels, layer_tail(): pl.pallas_call(functools.partial(tail_kernel, dims), name='layer_tail', o...  749 us
    dot_general x1, matrix products, attention_block(): jnp.einsum('bsd,dn->bsn', h_in, w_q, preferred_element_type=jnp.float32)  24.3 us

profile of v1, /device:TPU:0, one launch (start us, length us, event | category | flops | bytes accessed | tf_op | source)
XLA Modules:
  0.0 823.9 jit_solution(9056682456894307566)
XLA Ops:
  0.6 0.7 convert_element_type.56
  1.3 4.7 convert_reduce_fusion
  6.0 1.0 copy-done
  7.1 2.3 fusion.5
  9.5 0.6 reshape.180
  10.1 0.6 reshape.182
  10.7 0.3 multiply_cosine_fusion
  11.1 5.0 convert_reduce_fusion.1
  16.1 0.1 multiply_reduce_fusion.1
  16.2 3.7 fusion.33
  19.9 3.5 fusion.27
  23.5 0.2 copy.56
  23.7 0.3 subtract_convert_fusion.1
  24.0 0.1 slice.50
  24.2 24.3 %fusion.14 = bf16[4,128,2048]{2,1,0:T(8,128)(2,1)S(1)} fusion(bf16[8192,2048]{1,0:T(8,128)(2,1)} %param.16, bf16[4,128,8192]{2,1,0:T(8,128)(2,1)} %param.12, f32[8192]{0:T(1024)S(1)} %convert_element_type.51, f32[8192]{0:T(1024)S(1)} %convert_add_fusion, f32[4,128]{1,0:T(4,128)S(1)} %add_rsqrt_fusion, f32[4,128]{1,0:T(4,128)S(1)} %broadcast_multiply_fusion), kind=kOutput, calls=%fused_computation.23 | convolution fusion | flops 17206083584 | bytes 44109824 | tf_op jit(solution)/shard_map/bsd,dn->bsn/dot_general | solution.py:53
  48.5 0.6 copy.58
  49.1 0.6 slice.53
  49.8 0.5 copy.68
  50.3 0.6 copy_convert_fusion
  50.9 1.5 subtract_convert_fusion
  52.4 2.6 fusion.17
  55.0 1.1 fusion.50
  56.1 2.2 multiply_reduce_fusion
  58.3 0.1 sqrt_reduce_fusion
  58.5 0.7 reshape.178.pay_in
  59.2 3.4 copy.51
  62.7 2.3 reshape.172.attn_hbm
  65.0 749.0 %layer_tail.1 = (bf16[512,8192]{1,0:T(8,128)(2,1)}, f32[1,16512]{1,0:T(1,128)}) custom-call(bf16[512,2048]{1,0:T(8,128)(2,1)} %reshape.172.attn_hbm, bf16[512,8192]{1,0:T(8,128)(2,1)} %bitcast.61, bf16[2048,8192]{1,0:T(8,128)(2,1)} %wo_hbm.1, bf16[8192,8192]{1,0:T(8,128)(2,1)} %wup_hbm.1, bf16[8192,8192]{1,0:T(8,128)(2,1)} %wdn_hbm.1, f32[1,8192]{1,0:T(1,128)} %bitcast.67, ...), custom_call_target="tpu_custom_call" | custom-call | flops 154618822656 | bytes 570425344 | tf_op jit(solution)/shard_map/layer_tail/pallas_call | solution.py:443
  814.0 1.0 sqrt.10
  815.0 0.5 slice_bitcast_fusion
  815.5 0.6 fusion.49
  816.1 7.8 copy.70
  (25 shorter events, 0.4 us)
Async XLA Ops:
  1.3 5.8 copy-start
  7.1 2.4 copy-start.1
  7.1 2.4 copy-start.2
  7.1 2.4 copy-start.3
  7.1 3.0 copy-start.4
  11.1 5.1 copy-start.5
  16.2 3.7 copy-start.6

commit v2 on v1

v2 whole, which is shorter than its diff:
```python
import functools

import jax
import jax.numpy as jnp
from jax import lax
from jax.experimental import pallas as pl
from jax.experimental.pallas import tpu as pltpu
from jax.sharding import PartitionSpec as P

HEAD_DIM = 128
ROT_DIM = 64
ROPE_BASE = 10000.0
LN_EPS = 1e-5
MESH = pl.DeviceIdType.MESH

ITEM_COLS = 256
SKEW = 2
SLOTS = 8
LN_PARTS = 4
VMEM_BYTES = 52 << 20
LN1_AT = 8


def rope_tables(positions):
    rot_half = ROT_DIM // 2
    lane_id = jnp.arange(HEAD_DIM)
    pair = (lane_id % rot_half).astype(jnp.float32)
    inv_freq = ROPE_BASE ** (-2.0 * pair / ROT_DIM)
    pos_angle = positions.astype(jnp.float32)[:, None] * inv_freq[None, :]
    sign = jnp.where(lane_id < rot_half, -1.0, 1.0)
    return jnp.cos(pos_angle), jnp.sin(pos_angle) * sign[None, :]


def layer_kernel(
    dims,
    x_hbm, wq_hbm, wk_hbm, wv_hbm, wo_hbm, wup_hbm, wdn_hbm, gain1_ref, bias1_ref, gain2_ref, bias2_ref, cos_ref, sin_ref,
    xbuf, score_ref,
    attn, kbuf, vbuf, gains, biases, part, lhs, wbuf, rslot, bslot, acc8, pay, recvpay,
    in_sem, w_sem, r_send, r_recv, b_send, b_recv, p_send, p_recv, r_cred, b_cred,
):
    tp, dp, n_seq, width, k_attn, kv_width, n_items = dims
    n_chunks = 2
    z = lax.axis_index("tp")
    d = lax.axis_index("dp")
    last = tp - 1
    cw = width // n_items
    bw = 2 * cw
    n_blk = width // bw
    rows = 2 * n_seq
    total = 2 * n_chunks * n_items
    lag = 2 * last * SKEW

    barrier = pltpu.get_barrier_semaphore()
    for o in range(1, tp):
        pl.semaphore_signal(barrier, inc=1, device_id={"tp": lax.rem(z + o, tp)}, device_id_type=MESH)
    for o in range(1, dp):
        pl.semaphore_signal(barrier, inc=1, device_id={"dp": lax.rem(d + o, dp)}, device_id_type=MESH)

    def x_copy(c):
        r = pl.ds(c * rows, rows)
        return pltpu.make_async_copy(x_hbm.at[r, :], xbuf.at[r, :], in_sem.at[c])

    heads_blk = bw // HEAD_DIM
    n_q = k_attn // bw
    n_pre = 1 + n_q
    att_len = n_pre + n_blk
    n_att = n_chunks * att_len
    q_group = k_attn // kv_width

    def w_copy(hbm, b, slot):
        cols = pl.ds(pl.multiple_of(b * bw, bw), bw)
        return pltpu.make_async_copy(hbm.at[:, cols], wbuf.at[slot], w_sem.at[slot])

    def wo_copy(b, slot):
        cols = pl.ds(pl.multiple_of(b * bw, bw), bw)
        return pltpu.make_async_copy(wo_hbm.at[:, cols], wbuf.at[slot, pl.ds(0, k_attn), :], w_sem.at[slot])

    def k_copy(slot):
        return pltpu.make_async_copy(wk_hbm, wbuf.at[slot, :, pl.ds(0, kv_width)], w_sem.at[slot])

    def v_copy(slot):
        return pltpu.make_async_copy(wv_hbm, wbuf.at[slot, :, pl.ds(kv_width, kv_width)], w_sem.at[2])

    def start_block(idx):
        slot = lax.rem(idx, 2)

        @pl.when(idx < n_att)
        def _():
            j = lax.rem(idx, att_len)

            @pl.when(j == 0)
            def _():
                k_copy(slot).start()
                v_copy(slot).start()

            @pl.when((j > 0) & (j < n_pre))
            def _():
                w_copy(wq_hbm, j - 1, slot).start()

            @pl.when(j >= n_pre)
            def _():
                wo_copy(j - n_pre, slot).start()

        @pl.when((idx >= n_att) & (idx < n_att + n_mlp))
        def _():
            kk = lax.rem(idx - n_att, 2 * n_blk)

            @pl.when(kk < n_blk)
            def _():
                w_copy(wup_hbm, kk, slot).start()

            @pl.when(kk >= n_blk)
            def _():
                w_copy(wdn_hbm, kk - n_blk, slot).start()

    def rotate(heads):
        reps = heads.shape[0] // n_seq
        lane_id = lax.broadcasted_iota(jnp.int32, heads.shape, 1)
        quarter = ROT_DIM // 2
        partner = jnp.where(
            lane_id < quarter, pltpu.roll(heads, HEAD_DIM - quarter, 1), pltpu.roll(heads, quarter, 1)
        )
        cos_t = jnp.concatenate([cos_ref[...]] * reps, axis=0)
        sin_t = jnp.concatenate([sin_ref[...]] * reps, axis=0)
        return jnp.where(lane_id < ROT_DIM, heads * cos_t + partner * sin_t, heads).astype(jnp.bfloat16)

    def keys_values(slot):
        k_copy(slot).wait()
        v_copy(slot).wait()
        acc = jnp.dot(lhs[0], wbuf[slot], preferred_element_type=jnp.float32).astype(jnp.bfloat16)
        for g in range(2):
            r = slice(g * n_seq, (g + 1) * n_seq)
            for h in range(kv_width // HEAD_DIM):
                cl = slice(h * HEAD_DIM, (h + 1) * HEAD_DIM)
                kbuf[g, h] = rotate(acc[r, cl].astype(jnp.float32))
                vbuf[g, h] = acc[r, kv_width + h * HEAD_DIM:kv_width + (h + 1) * HEAD_DIM]

    def queries(jq, slot):
        w_copy(wq_hbm, jq, slot).wait()
        acc = jnp.dot(lhs[0], wbuf[slot], preferred_element_type=jnp.float32).astype(jnp.bfloat16)
        kv = lax.div(jq * heads_blk, q_group)
        shape = (heads_blk * n_seq, n_seq)
        causal = lax.rem(lax.broadcasted_iota(jnp.int32, shape, 0), n_seq) >= lax.broadcasted_iota(jnp.int32, shape, 1)
        lane_id = lax.broadcasted_iota(jnp.int32, (1, HEAD_DIM), 1)
        head_sq = jnp.zeros((1, HEAD_DIM), jnp.float32)
        for g in range(2):
            r = slice(g * n_seq, (g + 1) * n_seq)
            heads = jnp.concatenate(
                [acc[r, h * HEAD_DIM:(h + 1) * HEAD_DIM].astype(jnp.float32) for h in range(heads_blk)], axis=0
            )
            q_rot = rotate(heads)
            logits = lax.dot_general(
                q_rot, kbuf[g, kv], (((1,), (1,)), ((), ())), preferred_element_type=jnp.float32
            ) * HEAD_DIM ** -0.5
            logits = jnp.where(causal, logits, -1e30)
            weights = jnp.exp(logits - jnp.max(logits, axis=-1, keepdims=True))
            prob = (weights / jnp.sum(weights, axis=-1, keepdims=True)).astype(jnp.bfloat16)
            out = jnp.dot(prob, vbuf[g, kv], preferred_element_type=jnp.float32).astype(jnp.bfloat16)
            wide = out.astype(jnp.float32)
            norm = jnp.sqrt(jnp.sum(wide * wide, axis=-1, keepdims=True))
            for h in range(heads_blk):
                hr = slice(h * n_seq, (h + 1) * n_seq)
                attn[r, pl.ds(pl.multiple_of(jq * bw + h * HEAD_DIM, HEAD_DIM), HEAD_DIM)] = out[hr]
                m = jnp.sum(norm[hr], axis=0, keepdims=True) * (1.0 / n_seq)
                head_sq = head_sq + jnp.where(lane_id == jq * heads_blk + h, m * m, 0.0)
        pay[:, 2 * width:2 * width + HEAD_DIM] = pay[:, 2 * width:2 * width + HEAD_DIM] + head_sq

    def out_proj(c, b, slot):
        wo_copy(b, slot).wait()
        acc = jnp.dot(attn[...], wbuf[slot, 0:k_attn, :], preferred_element_type=jnp.float32)
        for g in range(2):
            for half in range(2):
                part[(2 * c + g) * n_items + 2 * b + half] = acc[
                    g * n_seq:(g + 1) * n_seq, half * cw:(half + 1) * cw
                ]

    def att_block(idx):
        slot = lax.rem(idx, 2)
        c = lax.div(idx, att_len)
        j = lax.rem(idx, att_len)

        @pl.when(j == 0)
        def _():
            keys_values(slot)

        @pl.when((j > 0) & (j < n_pre))
        def _():
            queries(j - 1, slot)

        @pl.when(j >= n_pre)
        def _():
            out_proj(c, j - n_pre, slot)

        start_block(idx + 2)

    n_mlp = 2 * n_blk * n_chunks
    x_copy(0).start()
    start_block(jnp.int32(0))
    start_block(jnp.int32(1))
    x_copy(1).start()
    pay[...] = jnp.zeros_like(pay)
    for which, (gain, bias) in enumerate(((gain1_ref, bias1_ref), (gain2_ref, bias2_ref))):
        gains[which] = 1.0 + gain[...].astype(jnp.float32)
        biases[which] = bias[...].astype(jnp.float32)
    x_copy(0).wait()
    pl.semaphore_wait(barrier, tp - 1 + dp - 1)

    def tile_of(t, g):
        c = lax.rem(lax.div(t, n_items), n_chunks)
        i = lax.rem(t, n_items)
        row = pl.multiple_of((2 * c + g) * n_seq, n_seq)
        col = pl.multiple_of(i * cw, cw)
        return (2 * c + g) * n_items + i, pl.ds(row, n_seq), pl.ds(col, cw)

    def place(g):
        return z if g == 0 else last - z

    def onward(g):
        return {"tp": z + 1} if g == 0 else {"tp": z - 1}

    def backward(g):
        return {"tp": z - 1} if g == 0 else {"tp": z + 1}

    def r_copy(g, t, src):
        slot = lax.rem(t, SLOTS)
        return pltpu.make_async_remote_copy(
            src_ref=src, dst_ref=rslot.at[g, slot], send_sem=r_send.at[g, slot], recv_sem=r_recv.at[g, slot],
            device_id=onward(g), device_id_type=MESH,
        )

    def b_copy(g, t, src):
        slot = lax.rem(t, SLOTS)
        return pltpu.make_async_remote_copy(
            src_ref=src, dst_ref=bslot.at[g, slot], send_sem=b_send.at[g, slot], recv_sem=b_recv.at[g, slot],
            device_id=backward(g), device_id_type=MESH,
        )

    def r_arrive(g, t, p):
        slot = lax.rem(t, SLOTS)
        idx, rws, cls = tile_of(t, g)

        @pl.when((p == 1) | (p == 2))
        def _():
            r_copy(g, t, rslot.at[g, slot]).wait_recv()
            rslot[g, slot] = rslot[g, slot] + part[idx]

        @pl.when(p == last)
        def _():
            r_copy(g, t, rslot.at[g, slot]).wait_recv()
            new = (xbuf[rws, cls].astype(jnp.float32) + (rslot[g, slot] + part[idx])).astype(jnp.bfloat16)
            xbuf[rws, cls] = new
            rslot[g, slot] = new.astype(jnp.float32)

    def r_leave(g, t, p):
        slot = lax.rem(t, SLOTS)
        old = t - SKEW
        old_slot = lax.rem(old + SLOTS, SLOTS)
        idx, _, _ = tile_of(t, g)

        @pl.when((p == 0) & (t >= SLOTS))
        def _():
            r_copy(g, t, part.at[idx]).wait_send()

        @pl.when((p < last) & (t >= SLOTS))
        def _():
            pl.semaphore_wait(r_cred.at[g], 1)

        @pl.when(p == 0)
        def _():
            r_copy(g, t, part.at[idx]).start()

        @pl.when((p == 1) | (p == 2))
        def _():
            r_copy(g, t, rslot.at[g, slot]).start()

        @pl.when((p == last) & (t >= SLOTS))
        def _():
            pl.semaphore_wait(b_cred.at[g], 1)

        @pl.when(p == last)
        def _():
            b_copy(g, t, rslot.at[g, slot]).start()

        @pl.when(((p == 1) | (p == 2)) & (old >= 0))
        def _():
            r_copy(g, old, rslot.at[g, old_slot]).wait_send()

        @pl.when((p == last) & (old >= 0))
        def _():
            b_copy(g, old, rslot.at[g, old_slot]).wait_send()

        @pl.when((p > 0) & (old >= 0) & (old < total - SLOTS))
        def _():
            pl.semaphore_signal(r_cred.at[g], inc=1, device_id=backward(g), device_id_type=MESH)

    def b_step(g, t, p):
        slot = lax.rem(t, SLOTS)
        old = t - SKEW
        old_slot = lax.rem(old + SLOTS, SLOTS)
        _, rws, cls = tile_of(t, g)
        b_copy(g, t, bslot.at[g, slot]).wait_recv()

        @pl.when((p > 0) & (t >= SLOTS))
        def _():
            pl.semaphore_wait(b_cred.at[g], 1)

        @pl.when(p > 0)
        def _():
            b_copy(g, t, bslot.at[g, slot]).start()

        xbuf[rws, cls] = bslot[g, slot].astype(jnp.bfloat16)

        @pl.when((p > 0) & (old >= 0))
        def _():
            b_copy(g, old, bslot.at[g, old_slot]).wait_send()

        @pl.when((old >= 0) & (old < total - SLOTS))
        def _():
            pl.semaphore_signal(b_cred.at[g], inc=1, device_id=onward(g), device_id_type=MESH)

    def service(s):
        for g in range(2):
            p = place(g)
            t = s - SKEW * p

            @pl.when((t >= 0) & (t < total))
            def _(g=g, p=p, t=t):
                r_arrive(g, t, p)

        for g in range(2):
            p = place(g)
            t = s - SKEW * (2 * last - p)

            @pl.when((p < last) & (t >= 0) & (t < total))
            def _(g=g, p=p, t=t):
                b_step(g, t, p)

        for g in range(2):
            p = place(g)
            t = s - SKEW * p

            @pl.when((t >= 0) & (t < total))
            def _(g=g, p=p, t=t):
                r_leave(g, t, p)

    lane = 512 if width % 512 == 0 else 128
    n_lane = width // lane
    ln_rows = rows // LN_PARTS
    seq_parts = n_seq // ln_rows

    def ln_part(which, c, q):
        @pl.when(lax.rem(q, seq_parts) == 0)
        def _():
            acc8[...] = jnp.zeros_like(acc8)

        def group(r, carry):
            src = pl.ds(pl.multiple_of(c * rows + q * ln_rows + r * 16, 16), 16)
            dst = pl.ds(pl.multiple_of(q * ln_rows + r * 16, 16), 16)
            tot = jnp.zeros((16, lane), jnp.float32)
            for j in range(n_lane):
                tot = tot + xbuf[src, j * lane:(j + 1) * lane].astype(jnp.float32)
            mean = jnp.sum(tot, axis=-1, keepdims=True) * (1.0 / width)
            var = jnp.zeros((16, lane), jnp.float32)
            for j in range(n_lane):
                cen = xbuf[src, j * lane:(j + 1) * lane].astype(jnp.float32) - mean
                var = var + cen * cen
            rstd = lax.rsqrt(jnp.sum(var, axis=-1, keepdims=True) * (1.0 / width) + LN_EPS)
            for j in range(n_lane):
                for i in range(lane // 128):
                    at = j * lane + i * 128
                    row = slice(at // 128, at // 128 + 1)
                    cl = slice(at, at + 128)
                    cen = xbuf[src, cl].astype(jnp.float32) - mean
                    h = ((cen * rstd) * gains[which, row, :] + biases[which, row, :]).astype(jnp.bfloat16)
                    lhs[0, dst, cl] = h
                    hf = h.astype(jnp.float32)
                    acc8[:, cl] = acc8[:, cl] + (hf[0:8] + hf[8:16])
            return carry

        lax.fori_loop(0, ln_rows // 16, group, 0)

        @pl.when(lax.rem(q, seq_parts) == seq_parts - 1)
        def _():
            m = jnp.sum(acc8[...], axis=0, keepdims=True) * (1.0 / n_seq)
            pay[:, width:2 * width] = pay[:, width:2 * width] + m * m

    def mlp_block(k):
        slot = lax.rem(n_att + k, 2)
        kk = lax.rem(k, 2 * n_blk)
        c = lax.div(k, 2 * n_blk)
        second = lax.div(kk, n_blk)
        b = kk - second * n_blk
        w_copy(wup_hbm, b, slot).wait()
        acc = jnp.dot(lhs[second], wbuf[slot], preferred_element_type=jnp.float32)

        @pl.when(second == 0)
        def _():
            relu = jnp.maximum(acc, 0.0)
            act = relu * relu
            cols = pl.ds(pl.multiple_of(b * bw, bw), bw)
            m0 = jnp.sum(act[0:n_seq], axis=0, keepdims=True) * (1.0 / n_seq)
            m1 = jnp.sum(act[n_seq:rows], axis=0, keepdims=True) * (1.0 / n_seq)
            pay[:, cols] = pay[:, cols] + (m0 * m0 + m1 * m1)
            lhs[1, :, cols] = act.astype(jnp.bfloat16)

        @pl.when(second == 1)
        def _():
            for g in range(2):
                for half in range(2):
                    part[(2 * c + g) * n_items + 2 * b + half] = acc[
                        g * n_seq:(g + 1) * n_seq, half * cw:(half + 1) * cw
                    ]

        start_block(n_att + k + 2)

    def pay_copy(peer, src_d, o):
        return pltpu.make_async_remote_copy(
            src_ref=pay, dst_ref=recvpay.at[src_d], send_sem=p_send.at[o], recv_sem=p_recv.at[src_d],
            device_id={"dp": peer}, device_id_type=MESH,
        )

    first = -(n_pre + 1 + LN_PARTS)
    ln_at = n_items - 1 + lag
    mlp_at = ln_at + LN_PARTS
    pay_at = mlp_at + n_mlp - n_blk + 2

    def step(i, carry):
        s = i + first

        @pl.when(s >= 0)
        def _():
            service(s)

        starts = (first, LN1_AT, ln_at, ln_at + n_items)
        on = [(s >= at) & (s < at + LN_PARTS) for at in starts]

        @pl.when(on[0] | on[1] | on[2] | on[3])
        def _():
            at = jnp.where(on[0], starts[0], jnp.where(on[1], starts[1], jnp.where(on[2], starts[2], starts[3])))
            ln_part(jnp.where(on[2] | on[3], 1, 0), jnp.where(on[1] | on[3], 1, 0), s - at)

        @pl.when(s == 0)
        def _():
            x_copy(1).wait()

        idx = s - first - LN_PARTS

        @pl.when((idx >= 0) & (idx < n_att))
        def _():
            att_block(idx)

        k = s - mlp_at

        @pl.when((k >= 0) & (k < n_mlp))
        def _():
            mlp_block(k)

        @pl.when(s == pay_at)
        def _():
            for o in range(1, dp):
                pay_copy(lax.rem(d + o, dp), d, o).start()
            recvpay[d] = pay[...]

        return carry

    lax.fori_loop(0, total + lag - first, step, 0)

    for o in range(1, dp):
        src_d = lax.rem(d + o, dp)
        pay_copy(src_d, src_d, o).wait_recv()
    score = recvpay[0]
    for j in range(1, dp):
        score = score + recvpay[j]
    score_ref[...] = jnp.sqrt(score)
    for o in range(1, dp):
        pay_copy(lax.rem(d + o, dp), d, o).wait_send()
    for g in range(2):
        p = place(g)
        for back in range(SLOTS):
            t = total - 1 - back
            slot = t % SLOTS

            @pl.when(p == 0)
            def _(g=g, t=t, slot=slot):
                r_copy(g, t, part.at[0]).wait_send()

            if back < SKEW:
                @pl.when((p == 1) | (p == 2))
                def _(g=g, t=t, slot=slot):
                    r_copy(g, t, rslot.at[g, slot]).wait_send()
                    b_copy(g, t, bslot.at[g, slot]).wait_send()

                @pl.when(p == last)
                def _(g=g, t=t, slot=slot):
                    b_copy(g, t, rslot.at[g, slot]).wait_send()


def layer(tp, dp, n_seq, x_rows, w_q, w_k, w_v, w_o, w_up, w_down, norms, rope):
    tokens, width = x_rows.shape
    k_attn = w_q.shape[1]
    kv_width = w_k.shape[1]
    cw = ITEM_COLS
    n_items = width // cw
    dims = (tp, dp, n_seq, width, k_attn, kv_width, n_items)
    rows = 2 * n_seq
    pay = (1, 2 * width + HEAD_DIM)
    hbm = pl.BlockSpec(memory_space=pl.ANY)
    vmem = pl.BlockSpec(memory_space=pltpu.VMEM)
    dma = pltpu.SemaphoreType.DMA
    return pl.pallas_call(
        functools.partial(layer_kernel, dims),
        name="layer",
        out_shape=(
            pltpu.VMEM((tokens, width), jnp.bfloat16),
            pltpu.VMEM(pay, jnp.float32),
        ),
        in_specs=[hbm] * 7 + [vmem] * 6,
        out_specs=(vmem, vmem),
        scratch_shapes=[
            pltpu.VMEM((rows, k_attn), jnp.bfloat16),
            pltpu.VMEM((2, kv_width // HEAD_DIM, n_seq, HEAD_DIM), jnp.bfloat16),
            pltpu.VMEM((2, kv_width // HEAD_DIM, n_seq, HEAD_DIM), jnp.bfloat16),
            pltpu.VMEM((2, width // 128, 128), jnp.float32),
            pltpu.VMEM((2, width // 128, 128), jnp.float32),
            pltpu.VMEM((tokens // n_seq * n_items, n_seq, cw), jnp.float32),
            pltpu.VMEM((2, rows, width), jnp.bfloat16),
            pltpu.VMEM((2, width, 2 * cw), jnp.bfloat16),
            pltpu.VMEM((2, SLOTS, n_seq, cw), jnp.float32),
            pltpu.VMEM((2, SLOTS, n_seq, cw), jnp.float32),
            pltpu.VMEM((8, width), jnp.float32),
            pltpu.VMEM(pay, jnp.float32),
            pltpu.VMEM((dp,) + pay, jnp.float32),
            dma((2,)), dma((3,)),
            dma((2, SLOTS)), dma((2, SLOTS)), dma((2, SLOTS)), dma((2, SLOTS)),
            dma((dp,)), dma((dp,)),
            pltpu.SemaphoreType.REGULAR((2,)), pltpu.SemaphoreType.REGULAR((2,)),
        ],
        compiler_params=pltpu.CompilerParams(
            collective_id=0, has_side_effects=True, vmem_limit_bytes=VMEM_BYTES
        ),
        cost_estimate=pl.CostEstimate(
            flops=4 * tokens * width * (k_attn + kv_width + width),
            bytes_accessed=4 * width * (2 * k_attn + 2 * kv_width + 2 * width),
            transcendentals=0,
        ),
    )(x_rows, w_q, w_k, w_v, w_o, w_up, w_down, *norms, *rope)


def solution(mesh):
    tp = mesh.shape["tp"]
    dp = mesh.shape["dp"]

    def local_layer(hidden, positions, ln1_gain, ln1_bias, w_q, w_k, w_v, w_o, ln2_gain, ln2_bias, w_up, w_down):
        n_batch, n_seq, width = hidden.shape
        ff_local = w_up.shape[1]
        heads = w_q.shape[1] // HEAD_DIM
        y_rows, score = layer(
            tp, dp, n_seq, hidden.reshape(n_batch * n_seq, width), w_q, w_k, w_v, w_o, w_up, w_down,
            [v.reshape(width // 128, 128) for v in (ln1_gain, ln1_bias, ln2_gain, ln2_bias)],
            rope_tables(positions),
        )
        roots = score.reshape(-1)
        return (
            y_rows.reshape(n_batch, n_seq, width),
            roots[:ff_local],
            roots[ff_local + width:ff_local + width + heads],
            roots[ff_local:ff_local + width],
        )

    weight_col = P(None, "tp")
    weight_row = P("tp", None)
    return jax.shard_map(
        local_layer,
        mesh=mesh,
        in_specs=(P("dp"), P(), P(), P(), weight_col, weight_col, weight_col, weight_row, P(), P(), weight_col, weight_row),
        out_specs=(P("dp"), P("tp"), P("tp"), P()),
        check_vma=False,
    )
```

time: 824 us -> 774 us (0.939)
  matrix products: 36.4 us -> 0 us
  Pallas kernels: 749 us -> 767 us
  other arithmetic: 18 us -> 1.64 us
  local copies, waits for them, and re-layouts: 19.7 us -> 4.54 us
    dot_general x5 -> x0, matrix products: 36.4 us -> none  [the longest x1 24.3 us: attention_block(): jnp.einsum('bsd,dn->bsn', h_in, w_q, preferred_element_type=jnp.float32)]
    pallas_call x1, Pallas kernels: 749 us -> 767 us  [layer(): pl.pallas_call(functools.partial(layer_kernel, dims), name='layer', out_s...]
    reduce_sum x6 -> x0, other arithmetic: 12.3 us -> none  [the longest x1 5 us: local_layer(): jnp.mean(h_in, axis=1, dtype=jnp.float32)]
where the time goes in v2:
time: 774 us
  Pallas kernels  767 us (99%)
    pallas_call x1, Pallas kernels, layer(): pl.pallas_call(functools.partial(layer_kernel, dims), name='layer', out_s...  767 us

profile of v2, /device:TPU:0, one launch (start us, length us, event | category | flops | bytes accessed | tf_op | source)
XLA Modules:
  0.0 773.8 jit_solution(16757328994212231469)
XLA Ops:
  0.6 0.7 convert_element_type.10
  1.3 1.0 fusion
  2.3 767.0 %layer.1 = (bf16[512,8192]{1,0:T(8,128)(2,1)S(1)}, f32[1,16512]{1,0:T(1,128)S(1)}) custom-call(bf16[512,8192]{1,0:T(8,128)(2,1)} %bitcast.13, bf16[8192,2048]{1,0:T(8,128)(2,1)} %wq_hbm.1, bf16[8192,256]{1,0:T(8,128)(2,1)} %wk_hbm.1, bf16[8192,256]{1,0:T(8,128)(2,1)} %wv_hbm.1, bf16[2048,8192]{1,0:T(8,128)(2,1)} %wo_hbm.1, bf16[8192,8192]{1,0:T(8,128)(2,1)} %wup_hbm.1, ...), custom_call_target="tpu_custom_call" | custom-call | flops 176093659136 | bytes 687865856 | tf_op jit(solution)/shard_map/layer/pallas_call | solution.py:510
  769.3 3.4 copy.17
  772.7 0.5 slice_bitcast_fusion
  773.2 0.6 fusion.4
  (1 shorter events, 0.0 us)

commit v3 on v2

--- a/solution.py
+++ b/solution.py
@@ -13,7 +13,9 @@
 LN_EPS = 1e-5
 MESH = pl.DeviceIdType.MESH
 
-ITEM_COLS = 256
+BLOCK_COLS = 512
+ITEM_COLS = 128
+TURNS = 2
 SKEW = 2
 SLOTS = 8
 LN_PARTS = 4
@@ -35,7 +37,7 @@
     dims,
     x_hbm, wq_hbm, wk_hbm, wv_hbm, wo_hbm, wup_hbm, wdn_hbm, gain1_ref, bias1_ref, gain2_ref, bias2_ref, cos_ref, sin_ref,
     xbuf, score_ref,
-    attn, kbuf, vbuf, gains, biases, part, lhs, wbuf, rslot, bslot, acc8, pay, recvpay,
+    attn, kbuf, vbuf, gains, biases, part, lhs, wbuf, rslot, bslot, pay, recvpay,
     in_sem, w_sem, r_send, r_recv, b_send, b_recv, p_send, p_recv, r_cred, b_cred,
 ):
     tp, dp, n_seq, width, k_attn, kv_width, n_items = dims
@@ -44,7 +46,8 @@
     d = lax.axis_index("dp")
     last = tp - 1
     cw = width // n_items
-    bw = 2 * cw
+    bw = BLOCK_COLS
+    per = bw // cw
     n_blk = width // bw
     rows = 2 * n_seq
     total = 2 * n_chunks * n_items
@@ -56,9 +59,14 @@
     for o in range(1, dp):
         pl.semaphore_signal(barrier, inc=1, device_id={"dp": lax.rem(d + o, dp)}, device_id_type=MESH)
 
-    def x_copy(c):
-        r = pl.ds(c * rows, rows)
-        return pltpu.make_async_copy(x_hbm.at[r, :], xbuf.at[r, :], in_sem.at[c])
+    ln_rows = rows // LN_PARTS
+
+    def x_copy(q):
+        r = pl.ds(pl.multiple_of(q * ln_rows, ln_rows), ln_rows)
+        return pltpu.make_async_copy(x_hbm.at[r, :], xbuf.at[r, :], in_sem.at[q])
+
+    rest = pl.ds(rows, rows)
+    x_rest = pltpu.make_async_copy(x_hbm.at[rest, :], xbuf.at[rest, :], in_sem.at[LN_PARTS])
 
     heads_blk = bw // HEAD_DIM
     n_q = k_attn // bw
@@ -141,8 +149,6 @@
         kv = lax.div(jq * heads_blk, q_group)
         shape = (heads_blk * n_seq, n_seq)
         causal = lax.rem(lax.broadcasted_iota(jnp.int32, shape, 0), n_seq) >= lax.broadcasted_iota(jnp.int32, shape, 1)
-        lane_id = lax.broadcasted_iota(jnp.int32, (1, HEAD_DIM), 1)
-        head_sq = jnp.zeros((1, HEAD_DIM), jnp.float32)
         for g in range(2):
             r = slice(g * n_seq, (g + 1) * n_seq)
             heads = jnp.concatenate(
@@ -156,23 +162,46 @@
             weights = jnp.exp(logits - jnp.max(logits, axis=-1, keepdims=True))
             prob = (weights / jnp.sum(weights, axis=-1, keepdims=True)).astype(jnp.bfloat16)
             out = jnp.dot(prob, vbuf[g, kv], preferred_element_type=jnp.float32).astype(jnp.bfloat16)
-            wide = out.astype(jnp.float32)
-            norm = jnp.sqrt(jnp.sum(wide * wide, axis=-1, keepdims=True))
             for h in range(heads_blk):
-                hr = slice(h * n_seq, (h + 1) * n_seq)
-                attn[r, pl.ds(pl.multiple_of(jq * bw + h * HEAD_DIM, HEAD_DIM), HEAD_DIM)] = out[hr]
-                m = jnp.sum(norm[hr], axis=0, keepdims=True) * (1.0 / n_seq)
-                head_sq = head_sq + jnp.where(lane_id == jq * heads_blk + h, m * m, 0.0)
-        pay[:, 2 * width:2 * width + HEAD_DIM] = pay[:, 2 * width:2 * width + HEAD_DIM] + head_sq
+                cl = pl.ds(pl.multiple_of(jq * bw + h * HEAD_DIM, HEAD_DIM), HEAD_DIM)
+                attn[r, cl] = out[h * n_seq:(h + 1) * n_seq]
+
+    def head_scores():
+        lane_id = lax.broadcasted_iota(jnp.int32, (1, HEAD_DIM), 1)
+
+        def some_heads(j, head_sq):
+            for h in range(heads_blk):
+                head = j * heads_blk + h
+                cl = pl.ds(pl.multiple_of(head * HEAD_DIM, HEAD_DIM), HEAD_DIM)
+                for g in range(2):
+                    wide = attn[g * n_seq:(g + 1) * n_seq, cl].astype(jnp.float32)
+                    norm = jnp.sqrt(jnp.sum(wide * wide, axis=-1, keepdims=True))
+                    m = jnp.sum(norm, axis=0, keepdims=True) * (1.0 / n_seq)
+                    head_sq = head_sq + jnp.where(lane_id == head, m * m, 0.0)
+            return head_sq
+
+        at = slice(2 * width, 2 * width + HEAD_DIM)
+        pay[:, at] = pay[:, at] + lax.fori_loop(0, n_q, some_heads, jnp.zeros((1, HEAD_DIM), jnp.float32))
+
+    def embed_scores():
+        def some_columns(j, carry):
+            cl = pl.ds(pl.multiple_of(j * bw, bw), bw)
+            m = [
+                jnp.sum(lhs[0, g * n_seq:(g + 1) * n_seq, cl].astype(jnp.float32), axis=0, keepdims=True) * (1.0 / n_seq)
+                for g in range(2)
+            ]
+            out = pl.ds(pl.multiple_of(width + j * bw, bw), bw)
+            pay[:, out] = pay[:, out] + (m[0] * m[0] + m[1] * m[1])
+            return carry
+
+        lax.fori_loop(0, n_blk, some_columns, 0)
 
     def out_proj(c, b, slot):
         wo_copy(b, slot).wait()
         acc = jnp.dot(attn[...], wbuf[slot, 0:k_attn, :], preferred_element_type=jnp.float32)
         for g in range(2):
-            for half in range(2):
-                part[(2 * c + g) * n_items + 2 * b + half] = acc[
-                    g * n_seq:(g + 1) * n_seq, half * cw:(half + 1) * cw
-                ]
+            for q in range(per):
+                part[(2 * c + g) * n_items + per * b + q] = acc[g * n_seq:(g + 1) * n_seq, q * cw:(q + 1) * cw]
 
     def att_block(idx):
         slot = lax.rem(idx, 2)
@@ -194,15 +223,15 @@
         start_block(idx + 2)
 
     n_mlp = 2 * n_blk * n_chunks
-    x_copy(0).start()
+    for q in range(LN_PARTS):
+        x_copy(q).start()
     start_block(jnp.int32(0))
     start_block(jnp.int32(1))
-    x_copy(1).start()
+    x_rest.start()
     pay[...] = jnp.zeros_like(pay)
     for which, (gain, bias) in enumerate(((gain1_ref, bias1_ref), (gain2_ref, bias2_ref))):
         gains[which] = 1.0 + gain[...].astype(jnp.float32)
         biases[which] = bias[...].astype(jnp.float32)
-    x_copy(0).wait()
     pl.semaphore_wait(barrier, tp - 1 + dp - 1)
 
     def tile_of(t, g):
@@ -345,14 +374,8 @@
 
     lane = 512 if width % 512 == 0 else 128
     n_lane = width // lane
-    ln_rows = rows // LN_PARTS
-    seq_parts = n_seq // ln_rows
 
     def ln_part(which, c, q):
-        @pl.when(lax.rem(q, seq_parts) == 0)
-        def _():
-            acc8[...] = jnp.zeros_like(acc8)
-
         def group(r, carry):
             src = pl.ds(pl.multiple_of(c * rows + q * ln_rows + r * 16, 16), 16)
             dst = pl.ds(pl.multiple_of(q * ln_rows + r * 16, 16), 16)
@@ -373,16 +396,9 @@
                     cen = xbuf[src, cl].astype(jnp.float32) - mean
                     h = ((cen * rstd) * gains[which, row, :] + biases[which, row, :]).astype(jnp.bfloat16)
                     lhs[0, dst, cl] = h
-                    hf = h.astype(jnp.float32)
-                    acc8[:, cl] = acc8[:, cl] + (hf[0:8] + hf[8:16])
             return carry
 
         lax.fori_loop(0, ln_rows // 16, group, 0)
-
-        @pl.when(lax.rem(q, seq_parts) == seq_parts - 1)
-        def _():
-            m = jnp.sum(acc8[...], axis=0, keepdims=True) * (1.0 / n_seq)
-            pay[:, width:2 * width] = pay[:, width:2 * width] + m * m
 
     def mlp_block(k):
         slot = lax.rem(n_att + k, 2)
@@ -406,10 +422,8 @@
         @pl.when(second == 1)
         def _():
             for g in range(2):
-                for half in range(2):
-                    part[(2 * c + g) * n_items + 2 * b + half] = acc[
-                        g * n_seq:(g + 1) * n_seq, half * cw:(half + 1) * cw
-                    ]
+                for q in range(per):
+                    part[(2 * c + g) * n_items + per * b + q] = acc[g * n_seq:(g + 1) * n_seq, q * cw:(q + 1) * cw]
 
         start_block(n_att + k + 2)
 
@@ -420,19 +434,31 @@
         )
 
     first = -(n_pre + 1 + LN_PARTS)
-    ln_at = n_items - 1 + lag
+    span = n_items // TURNS
+    ln_at = -(-(n_items - TURNS + lag) // TURNS)
     mlp_at = ln_at + LN_PARTS
     pay_at = mlp_at + n_mlp - n_blk + 2
 
-    def step(i, carry):
-        s = i + first
-
-        @pl.when(s >= 0)
-        def _():
-            service(s)
-
-        starts = (first, LN1_AT, ln_at, ln_at + n_items)
+    def turn(i, carry):
+        u = i + first * TURNS
+
+        @pl.when(u >= 0)
+        def _():
+            service(u)
+
+        @pl.when(lax.rem(i, TURNS) == TURNS - 1)
+        def _():
+            step(lax.div(i, TURNS) + first)
+
+        return carry
+
+    def step(s):
+        starts = (first, LN1_AT, ln_at, ln_at + span)
         on = [(s >= at) & (s < at + LN_PARTS) for at in starts]
+
+        @pl.when(on[0])
+        def _():
+            x_copy(s - first).wait()
 
         @pl.when(on[0] | on[1] | on[2] | on[3])
         def _():
@@ -441,7 +467,15 @@
 
         @pl.when(s == 0)
         def _():
-            x_copy(1).wait()
+            x_rest.wait()
+
+        @pl.when((s == LN1_AT - 2) | (s == LN1_AT + LN_PARTS) | (s == mlp_at) | (s == mlp_at + span))
+        def _():
+            embed_scores()
+
+        @pl.when((s == LN1_AT + LN_PARTS + 1) | (s == n_att - n_pre - 1))
+        def _():
+            head_scores()
 
         idx = s - first - LN_PARTS
 
@@ -461,9 +495,7 @@
                 pay_copy(lax.rem(d + o, dp), d, o).start()
             recvpay[d] = pay[...]
 
-        return carry
-
-    lax.fori_loop(0, total + lag - first, step, 0)
+    lax.fori_loop(0, total + lag - first * TURNS, turn, 0)
 
     for o in range(1, dp):
         src_d = lax.rem(d + o, dp)
@@ -524,13 +556,12 @@
             pltpu.VMEM((2, width // 128, 128), jnp.float32),
             pltpu.VMEM((tokens // n_seq * n_items, n_seq, cw), jnp.float32),
             pltpu.VMEM((2, rows, width), jnp.bfloat16),
-            pltpu.VMEM((2, width, 2 * cw), jnp.bfloat16),
+            pltpu.VMEM((2, width, BLOCK_COLS), jnp.bfloat16),
             pltpu.VMEM((2, SLOTS, n_seq, cw), jnp.float32),
             pltpu.VMEM((2, SLOTS, n_seq, cw), jnp.float32),
-            pltpu.VMEM((8, width), jnp.float32),
             pltpu.VMEM(pay, jnp.float32),
             pltpu.VMEM((dp,) + pay, jnp.float32),
-            dma((2,)), dma((3,)),
+            dma((LN_PARTS + 1,)), dma((3,)),
             dma((2, SLOTS)), dma((2, SLOTS)), dma((2, SLOTS)), dma((2, SLOTS)),
             dma((dp,)), dma((dp,)),
             pltpu.SemaphoreType.REGULAR((2,)), pltpu.SemaphoreType.REGULAR((2,)),

time: 774 us -> 774 us (level)
  no operation moved by 1% of the time
where the time goes in v3:
time: 774 us
  Pallas kernels  767 us (99%)
    pallas_call x1, Pallas kernels, layer(): pl.pallas_call(functools.partial(layer_kernel, dims), name='layer', out_s...  767 us

profile of v3, /device:TPU:0, one launch (start us, length us, event | category | flops | bytes accessed | tf_op | source)
XLA Modules:
  0.0 773.7 jit_solution(5901876434505509946)
XLA Ops:
  0.6 0.7 convert_element_type.10
  1.3 1.0 fusion
  2.3 766.9 %layer.1 = (bf16[512,8192]{1,0:T(8,128)(2,1)S(1)}, f32[1,16512]{1,0:T(1,128)S(1)}) custom-call(bf16[512,8192]{1,0:T(8,128)(2,1)} %bitcast.13, bf16[8192,2048]{1,0:T(8,128)(2,1)} %wq_hbm.1, bf16[8192,256]{1,0:T(8,128)(2,1)} %wk_hbm.1, bf16[8192,256]{1,0:T(8,128)(2,1)} %wv_hbm.1, bf16[2048,8192]{1,0:T(8,128)(2,1)} %wo_hbm.1, bf16[8192,8192]{1,0:T(8,128)(2,1)} %wup_hbm.1, ...), custom_call_target="tpu_custom_call" | custom-call | flops 176093659136 | bytes 687865856 | tf_op jit(solution)/shard_map/layer/pallas_call | solution.py:542
  769.2 3.4 copy.17
  772.6 0.5 slice_bitcast_fusion
  773.1 0.6 fusion.4
  (1 shorter events, 0.0 us)

commit v4 on v3

--- a/solution.py
+++ b/solution.py
@@ -16,8 +16,8 @@
 BLOCK_COLS = 512
 ITEM_COLS = 128
 TURNS = 2
-SKEW = 2
-SLOTS = 8
+SKEW = 3
+SLOTS = 12
 LN_PARTS = 4
 VMEM_BYTES = 52 << 20
 LN1_AT = 8
@@ -225,9 +225,6 @@
     n_mlp = 2 * n_blk * n_chunks
     for q in range(LN_PARTS):
         x_copy(q).start()
-    start_block(jnp.int32(0))
-    start_block(jnp.int32(1))
-    x_rest.start()
     pay[...] = jnp.zeros_like(pay)
     for which, (gain, bias) in enumerate(((gain1_ref, bias1_ref), (gain2_ref, bias2_ref))):
         gains[which] = 1.0 + gain[...].astype(jnp.float32)
@@ -460,6 +457,14 @@
         def _():
             x_copy(s - first).wait()
 
+            @pl.when(s < first + 2)
+            def _():
+                start_block(s - first)
+
+            @pl.when(s == first + LN_PARTS - 1)
+            def _():
+                x_rest.start()
+
         @pl.when(on[0] | on[1] | on[2] | on[3])
         def _():
             at = jnp.where(on[0], starts[0], jnp.where(on[1], starts[1], jnp.where(on[2], starts[2], starts[3])))
@@ -495,15 +500,18 @@
                 pay_copy(lax.rem(d + o, dp), d, o).start()
             recvpay[d] = pay[...]
 
+        @pl.when(s == pay_at + 8)
+        def _():
+            for o in range(1, dp):
+                src_d = lax.rem(d + o, dp)
+                pay_copy(src_d, src_d, o).wait_recv()
+            score = recvpay[0]
+            for j in range(1, dp):
+                score = score + recvpay[j]
+            score_ref[...] = jnp.sqrt(score)
+
     lax.fori_loop(0, total + lag - first * TURNS, turn, 0)
 
-    for o in range(1, dp):
-        src_d = lax.rem(d + o, dp)
-        pay_copy(src_d, src_d, o).wait_recv()
-    score = recvpay[0]
-    for j in range(1, dp):
-        score = score + recvpay[j]
-    score_ref[...] = jnp.sqrt(score)
     for o in range(1, dp):
         pay_copy(lax.rem(d + o, dp), d, o).wait_send()
     for g in range(2):

time: 774 us -> 770 us (level)
  no operation moved by 1% of the time
where the time goes in v4:
time: 770 us
  Pallas kernels  763 us (99%)
    pallas_call x1, Pallas kernels, layer(): pl.pallas_call(functools.partial(layer_kernel, dims), name='layer', out_s...  763 us

profile of v4, /device:TPU:0, one launch (start us, length us, event | category | flops | bytes accessed | tf_op | source)
XLA Modules:
  0.0 769.7 jit_solution(5852748350954579920)
XLA Ops:
  0.6 0.7 convert_element_type.10
  1.3 1.0 fusion
  2.3 762.9 %layer.1 = (bf16[512,8192]{1,0:T(8,128)(2,1)S(1)}, f32[1,16512]{1,0:T(1,128)S(1)}) custom-call(bf16[512,8192]{1,0:T(8,128)(2,1)} %bitcast.13, bf16[8192,2048]{1,0:T(8,128)(2,1)} %wq_hbm.1, bf16[8192,256]{1,0:T(8,128)(2,1)} %wk_hbm.1, bf16[8192,256]{1,0:T(8,128)(2,1)} %wv_hbm.1, bf16[2048,8192]{1,0:T(8,128)(2,1)} %wo_hbm.1, bf16[8192,8192]{1,0:T(8,128)(2,1)} %wup_hbm.1, ...), custom_call_target="tpu_custom_call" | custom-call | flops 176093659136 | bytes 687865856 | tf_op jit(solution)/shard_map/layer/pallas_call | solution.py:550
  765.2 3.4 copy.17
  768.6 0.5 slice_bitcast_fusion
  769.1 0.6 fusion.4
  (1 shorter events, 0.0 us)
